TPU v7x, 32 devices: a whole 2x2x4 slice. The times are simulated.
32 devices in a mesh: dom: 8 (over z, x), sub: 4 (over y, core).
Axes of the slice: x: 2, y: 2, z: 4, core: 2. Of those that a mesh axis runs over, the one named last changes fastest.
Arguments:
- features: bfloat16 [32768, 256], P(('dom', 'sub')), may hold values from -16 to 16
- weight: bfloat16 [256, 256], replicated, may hold values from -0.375 to 0.375
- send_far: int32 [16384], P(('dom', 'sub')), may hold values from 0 to 1023
- send_near: int32 [4096], P(('dom', 'sub')), may hold values from 0 to 1023
- tile_dst: int32 [512], P(('dom', 'sub')), may hold values from 0 to 7
- inner_src: int32 [256], P(('dom', 'sub')), may hold values from 0 to 7
- outer_src: int32 [256], P(('dom', 'sub')), may hold values from 0 to 4
- tile_live: int32 [32, 2], P(('dom', 'sub')), may hold values from 4 to 8
- tile_weight: bfloat16 [512, 128, 128], P(('dom', 'sub')), may hold values from -0.3125 to 0.3125
Outputs:
- whitened: bfloat16 [32768, 256], P(('dom', 'sub'))
- loss_value: float32 [], replicated
Inputs may be any that keep to these rules, and one draw needn't show every extreme that they name: `send_far`: rows may repeat. `tile_live`: live slots come first in each half of a device's slots.
All inputs are finite; a program needn't handle non-finite values.
Results may differ from a plain program's by a relative error of at most 0.0085.
Values may be sent and summed in bfloat16 or wider, within the bound.
A program may use at most 64 MiB of HBM per device.

v0:
```python
import functools

import jax
import jax.numpy as jnp
from jax import lax
from jax.experimental import pallas as pl
from jax.experimental.pallas import tpu as pltpu
from jax.sharding import PartitionSpec as P

epsilon = 1e-05
MESH = pl.DeviceIdType.MESH
LEAF = 64
HIGH = lax.Precision.HIGHEST


def one_hot_rows(index_row, row_count):
    rows = index_row.shape[1]
    columns = jnp.broadcast_to(index_row, (128, rows)).T
    lane = lax.broadcasted_iota(jnp.int32, (rows, 128), 1)
    parts = [
        jnp.where(columns == lane + start, 1.0, 0.0).astype(jnp.bfloat16)
        for start in range(0, row_count, 128)
    ]
    return jnp.concatenate(parts, axis=1)


def padded_rows(count):
    return -(-count // 16) * 16


def packing(packed_rows, padded_total, n_dom, n_sub, per_dom, per_sub, near_rows_each):
    near_total = n_sub * near_rows_each
    far_total = packed_rows - near_total
    far_rows_each = far_total // n_dom
    row = lax.broadcasted_iota(jnp.int32, (packed_rows, padded_total), 0)
    column = lax.broadcasted_iota(jnp.int32, (packed_rows, padded_total), 1)
    far_place = row + lax.div(row, far_rows_each) * (per_dom - far_rows_each)
    near_row = row - far_total
    near_place = (
        n_dom * per_dom + near_row + lax.div(near_row, near_rows_each) * (per_sub - near_rows_each)
    )
    place = jnp.where(row < far_total, far_place, near_place)
    return jnp.where(place == column, 1.0, 0.0).astype(jnp.bfloat16)


def leaf_inverse(block):
    size = block.shape[0]
    row = lax.broadcasted_iota(jnp.int32, (size, size), 0)
    lane = lax.broadcasted_iota(jnp.int32, (size, size), 1)
    work = jnp.concatenate([block, jnp.where(row == lane, 1.0, 0.0)], axis=1)
    group = 8
    done = []
    for step in range(0, size, group):
        lines = [work[i : i + 1, :] for i in range(group)]
        entry = {
            (i, j): jnp.broadcast_to(lines[i][:, step + j : step + j + 1], (1, 2 * size))
            for i in range(group)
            for j in range(i, group)
        }
        inverse = []
        for i in range(group):
            inverse.append(1.0 / entry[i, i])
            for j in range(i + 1, group):
                share = entry[i, j] * inverse[i]
                for k in range(j, group):
                    entry[j, k] = entry[j, k] - share * entry[i, k]
                lines[j] = lines[j] - share * lines[i]
            done.append((lines[i] / jnp.sqrt(entry[i, i]))[:, size:])
        if step + group == size:
            break
        solved = [None] * group
        for i in reversed(range(group)):
            line = lines[i]
            for j in range(i + 1, group):
                line = line - entry[i, j] * solved[j]
            solved[i] = line * inverse[i]
        work = work[group:, :]
        update = work[:, step : step + 1] * solved[0]
        for i in range(1, group):
            update = update + work[:, step + i : step + i + 1] * solved[i]
        work = work - update
    return jnp.concatenate(done, axis=0)


def kernel(
    n_dom,
    n_sub,
    near_each,
    features_in,
    weight_in,
    far_in,
    near_in,
    dst_in,
    inner_in,
    outer_in,
    live_in,
    tile_in,
    out_ref,
    loss_ref,
    features_ref,
    weight_ref,
    far_ref,
    near_ref,
    dst_ref,
    inner_ref,
    outer_ref,
    live_ref,
    tile_ref,
    result,
    far_send,
    near_send,
    arrived,
    table,
    products,
    acc,
    aggregate,
    gram_part,
    gram_in,
    gram_own,
    gram,
    loss_own,
    loss_all,
    work,
    load_sems,
    halo_sems,
    sum_sems,
):
    total_devices = n_dom * n_sub
    dom = lax.axis_index("dom")
    sub = lax.axis_index("sub")
    me = dom * n_sub + sub
    tiles, size, feat = features_ref.shape
    rows = tiles * size
    slots = inner_ref.shape[0]
    share = gram_own.shape[0]
    owners = gram_part.shape[0] // share
    mine = lax.div(me * owners + total_devices - 1, total_devices)
    owns = jnp.logical_and(mine < owners, lax.div(mine * total_devices, owners) == me)

    def home(owner):
        return lax.div(owner * total_devices, owners)

    def share_rows(owner):
        return pl.ds(pl.multiple_of(owner * share, share), share)

    incoming = (
        (far_in, far_ref),
        (near_in, near_ref),
        (features_in, features_ref),
        (inner_in, inner_ref),
        (outer_in, outer_ref),
        (dst_in, dst_ref),
        (live_in, live_ref),
        (tile_in, tile_ref),
        (weight_in, weight_ref),
    )
    loads = [
        pltpu.make_async_copy(source, target, load_sems.at[place])
        for place, (source, target) in enumerate(incoming)
    ]

    def device_of(index):
        return (lax.div(index, n_sub), lax.rem(index, n_sub))

    barrier = pltpu.get_barrier_semaphore()

    @pl.loop(1, total_devices)
    def _(offset):
        peer = lax.rem(me + offset, total_devices)
        pl.semaphore_signal(barrier, inc=1, device_id=device_of(peer), device_id_type=MESH)

    for load in loads:
        load.start()
    for load in loads[:3]:
        load.wait()

    features = features_ref[...].reshape(rows, feat)
    far_rows = jnp.dot(
        one_hot_rows(far_ref[...], rows), features, preferred_element_type=jnp.float32
    ).astype(jnp.bfloat16)
    near_rows = jnp.dot(
        one_hot_rows(near_ref[...], rows), features, preferred_element_type=jnp.float32
    ).astype(jnp.bfloat16)
    far_send[...] = far_rows
    near_send[...] = near_rows
    per_dom = far_send.shape[0] // n_dom
    per_sub = near_send.shape[0] // n_sub
    far_count = per_dom * n_dom
    packed = size % per_dom == 0 and size % per_sub == 0 and arrived.shape[0] == table.shape[0] * size

    def place(first, count):
        if packed:
            within = pl.multiple_of(lax.rem(first, size), count)
            return table.at[lax.div(first, size), pl.ds(within, count)]
        return arrived.at[pl.ds(pl.multiple_of(first, count), count)]

    def dom_rows(index):
        return pl.ds(pl.multiple_of(index * per_dom, per_dom), per_dom)

    def sub_rows(index):
        return pl.ds(pl.multiple_of(index * per_sub, per_sub), per_sub)

    def dom_place(index):
        return place(index * per_dom, per_dom)

    def sub_place(index):
        return place(far_count + index * per_sub, per_sub)

    pl.semaphore_wait(barrier, total_devices - 1)

    @pl.loop(1, n_dom)
    def _(offset):
        peer = lax.rem(dom + offset, n_dom)
        pltpu.make_async_remote_copy(
            src_ref=far_send.at[dom_rows(peer)],
            dst_ref=dom_place(dom),
            send_sem=halo_sems.at[0],
            recv_sem=halo_sems.at[1],
            device_id=(peer, sub),
            device_id_type=MESH,
        ).start()

    @pl.loop(1, n_sub)
    def _(offset):
        peer = lax.rem(sub + offset, n_sub)
        pltpu.make_async_remote_copy(
            src_ref=near_send.at[sub_rows(peer)],
            dst_ref=sub_place(sub),
            send_sem=halo_sems.at[2],
            recv_sem=halo_sems.at[3],
            device_id=(dom, peer),
            device_id_type=MESH,
        ).start()

    dom_place(dom)[...] = far_send[dom_rows(dom), :]
    sub_place(sub)[...] = near_send[sub_rows(sub), :]

    def slot_products(rows_ref, source, first):
        for slot in range(slots):
            products[slot] = jnp.dot(
                tile_ref[first + slot],
                rows_ref[source[slot]],
                preferred_element_type=jnp.float32,
            )

    def slot_sum(tile, first, count):
        total = None
        for slot in range(slots):
            target = jnp.full((1, feat), dst_ref[first + slot], jnp.int32)
            chosen = jnp.where(jnp.logical_and(target == tile, count > slot), 1.0, 0.0)
            term = products[slot] * chosen
            total = term if total is None else total + term
        return total

    for load in loads[3:]:
        load.wait()
    slot_products(features_ref, inner_ref, 0)
    inner_count = jnp.full((1, feat), live_ref[0, 0], jnp.int32)
    outer_count = jnp.full((1, feat), live_ref[0, 1], jnp.int32)

    @pl.loop(0, tiles)
    def _(tile):
        acc[tile] = slot_sum(tile, 0, inner_count)

    def settle(ref, sem):
        pltpu.make_async_copy(ref, ref, sem).wait()

    settle(arrived.at[pl.ds(0, per_dom * (n_dom - 1))], halo_sems.at[1])
    settle(arrived.at[pl.ds(0, per_sub * (n_sub - 1))], halo_sems.at[3])
    if not packed:
        table[...] = jnp.dot(
            packing(table.shape[0] * size, arrived.shape[0], n_dom, n_sub, per_dom, per_sub, near_each),
            arrived[...],
            preferred_element_type=jnp.float32,
        ).astype(jnp.bfloat16).reshape(table.shape)
    slot_products(table, outer_ref, slots)

    @pl.loop(0, tiles)
    def _(tile):
        total = acc[tile] + slot_sum(tile, slots, outer_count)
        aggregate[pl.ds(pl.multiple_of(tile * size, size), size), :] = total.astype(jnp.bfloat16)

    projected = jnp.dot(aggregate[...], weight_ref[...], preferred_element_type=jnp.float32)
    hidden = (
        features_ref[...].reshape(rows, feat).astype(jnp.float32) + projected / (1.0 + jnp.exp(-projected))
    ).astype(jnp.bfloat16)
    hidden_t = hidden.T
    blocks = [(top, side) for top in range(0, feat, 128) for side in range(top, feat, 128)]
    for top in range(0, feat, 128):
        stripe = jnp.dot(
            hidden_t[top : top + 128, :], hidden[:, top:], preferred_element_type=jnp.float32
        )
        for side in range(top, feat, 128):
            at = 128 * blocks.index((top, side))
            gram_part[at : at + 128, :] = stripe[:, side - top : side - top + 128]

    @pl.loop(0, owners)
    def _(turn):
        owner = lax.rem(mine + turn, owners)
        peer = home(owner)

        @pl.when(peer != me)
        def _():
            pltpu.make_async_remote_copy(
                src_ref=gram_part.at[share_rows(owner)],
                dst_ref=gram_in.at[me],
                send_sem=sum_sems.at[0],
                recv_sem=sum_sems.at[1],
                device_id=device_of(peer),
                device_id_type=MESH,
            ).start()

    @pl.when(owns)
    def _():
        gram_in[me] = gram_part[share_rows(mine), :]
        settle(gram_in.at[pl.ds(0, total_devices - 1)], sum_sems.at[1])
        total = jnp.sum(gram_in[...], axis=0)
        gram_own[...] = total
        gram[share_rows(mine), :] = total

        @pl.loop(1, total_devices)
        def _(offset):
            peer = lax.rem(me + offset, total_devices)
            pltpu.make_async_remote_copy(
                src_ref=gram_own,
                dst_ref=gram.at[share_rows(mine)],
                send_sem=sum_sems.at[2],
                recv_sem=sum_sems.at[3],
                device_id=device_of(peer),
                device_id_type=MESH,
            ).start()

        settle(gram.at[pl.ds(0, share * (owners - 1))], sum_sems.at[3])

    @pl.when(jnp.logical_not(owns))
    def _():
        settle(gram, sum_sems.at[3])

    vertex_count = rows * total_devices
    diagonal = lax.broadcasted_iota(jnp.int32, (feat, feat), 0) == lax.broadcasted_iota(
        jnp.int32, (feat, feat), 1
    )
    identity = jnp.where(diagonal, 1.0, 0.0)
    for top, side in blocks:
        at = 128 * blocks.index((top, side))
        work[top : top + 128, side : side + 128] = (
            gram[at : at + 128, :] / vertex_count
            + epsilon * identity[top : top + 128, side : side + 128]
        )
        if side > top:
            work[side : side + 128, top : top + 128] = jnp.zeros((128, 128), jnp.float32)
    work[:, feat:] = identity
    for start in range(0, feat, LEAF):
        stop = start + LEAF
        inverse = leaf_inverse(work[start:stop, start:stop])
        pivot_rows = jnp.dot(
            inverse, work[start:stop, :], precision=HIGH, preferred_element_type=jnp.float32
        )
        work[start:stop, :] = pivot_rows
        if stop < feat:
            work[stop:, :] = work[stop:, :] - lax.dot_general(
                pivot_rows[:, stop:feat],
                pivot_rows,
                (((0,), (0,)), ((), ())),
                precision=HIGH,
                preferred_element_type=jnp.float32,
            )

    lower_inverse = work[:, feat:]
    high_part = lower_inverse.astype(jnp.bfloat16)
    low_part = (lower_inverse - high_part.astype(jnp.float32)).astype(jnp.bfloat16)
    across = (((1,), (1,)), ((), ()))
    white = lax.dot_general(
        hidden, high_part, across, preferred_element_type=jnp.float32
    ) + lax.dot_general(hidden, low_part, across, preferred_element_type=jnp.float32)
    result[...] = white.astype(jnp.bfloat16)
    store = pltpu.make_async_copy(result, out_ref, load_sems.at[len(loads)])
    store.start()

    distance = white - features_ref[...].reshape(rows, feat).astype(jnp.float32)
    wide = jnp.sum(distance * distance, axis=0, keepdims=True)
    partial = wide[:, :128]
    for side in range(128, feat, 128):
        partial = partial + wide[:, side : side + 128]
    loss_own[...] = partial
    loss_all[me] = partial

    @pl.loop(1, total_devices)
    def _(offset):
        peer = lax.rem(me + offset, total_devices)
        pltpu.make_async_remote_copy(
            src_ref=loss_own,
            dst_ref=loss_all.at[me],
            send_sem=sum_sems.at[4],
            recv_sem=sum_sems.at[5],
            device_id=device_of(peer),
            device_id_type=MESH,
        ).start()

    settle(far_send.at[pl.ds(0, per_dom * (n_dom - 1))], halo_sems.at[0])
    settle(near_send.at[pl.ds(0, per_sub * (n_sub - 1))], halo_sems.at[2])

    @pl.when(owns)
    def _():
        settle(gram_part.at[pl.ds(0, share * (owners - 1))], sum_sems.at[0])
        settle(gram_in.at[pl.ds(0, total_devices - 1)], sum_sems.at[2])

    @pl.when(jnp.logical_not(owns))
    def _():
        settle(gram_part, sum_sems.at[0])

    settle(loss_all.at[pl.ds(0, total_devices - 1)], sum_sems.at[4])
    settle(loss_all.at[pl.ds(0, total_devices - 1)], sum_sems.at[5])
    loss_ref[0, 0] = jnp.sum(jnp.sum(loss_all[...], axis=0)) / (vertex_count * feat)
    store.wait()


def body(
    n_dom,
    n_sub,
    features,
    weight,
    send_far,
    send_near,
    tile_dst,
    inner_src,
    outer_src,
    tile_live,
    tile_weight,
):
    rows, feat = features.shape
    size = tile_weight.shape[1]
    slots = inner_src.shape[0]
    total = n_dom * n_sub
    tiles_wide = feat // 128
    packed_rows = 128 * (tiles_wide * (tiles_wide + 1) // 2)
    share = 8
    while packed_rows % share or packed_rows // share > total:
        share += 8
    far_count = send_far.shape[0]
    near_count = send_near.shape[0]

    def padded(index, peers):
        each = index.shape[0] // peers
        grid = index.reshape(peers, each)
        return jnp.pad(grid, ((0, 0), (0, padded_rows(each) - each))).reshape(1, -1)

    far_index = padded(send_far, n_dom)
    near_index = padded(send_near, n_sub)
    far_padded = far_index.shape[1]
    near_padded = near_index.shape[1]
    anywhere = pl.BlockSpec(memory_space=pl.ANY)
    smem = pl.BlockSpec(memory_space=pltpu.SMEM)
    f32 = jnp.float32
    bf16 = jnp.bfloat16
    whitened, loss = pl.pallas_call(
        functools.partial(kernel, n_dom, n_sub, near_count // n_sub),
        out_shape=(
            jax.ShapeDtypeStruct((rows, feat), bf16),
            jax.ShapeDtypeStruct((1, 1), f32),
        ),
        in_specs=[anywhere] * 9,
        out_specs=(anywhere, smem),
        scratch_shapes=[
            pltpu.VMEM((rows // size, size, feat), bf16),
            pltpu.VMEM(weight.shape, bf16),
            pltpu.VMEM((1, far_padded), jnp.int32),
            pltpu.VMEM((1, near_padded), jnp.int32),
            pltpu.SMEM(tile_dst.shape, jnp.int32),
            pltpu.SMEM(inner_src.shape, jnp.int32),
            pltpu.SMEM(outer_src.shape, jnp.int32),
            pltpu.SMEM(tile_live.shape, jnp.int32),
            pltpu.VMEM(tile_weight.shape, bf16),
            pltpu.VMEM((rows, feat), bf16),
            pltpu.VMEM((far_padded, feat), bf16),
            pltpu.VMEM((near_padded, feat), bf16),
            pltpu.VMEM((far_padded + near_padded, feat), bf16),
            pltpu.VMEM(((far_count + near_count) // size, size, feat), bf16),
            pltpu.VMEM((slots, size, feat), f32),
            pltpu.VMEM((rows // size, size, feat), f32),
            pltpu.VMEM((rows, feat), bf16),
            pltpu.VMEM((packed_rows, 128), f32),
            pltpu.VMEM((total, share, 128), f32),
            pltpu.VMEM((share, 128), f32),
            pltpu.VMEM((packed_rows, 128), f32),
            pltpu.VMEM((1, 128), f32),
            pltpu.VMEM((total, 1, 128), f32),
            pltpu.VMEM((feat, 2 * feat), f32),
            pltpu.SemaphoreType.DMA((10,)),
            pltpu.SemaphoreType.DMA((4,)),
            pltpu.SemaphoreType.DMA((6,)),
        ],
        compiler_params=pltpu.CompilerParams(collective_id=0, has_side_effects=True),
    )(
        features.reshape(rows // size, size, feat),
        weight,
        far_index,
        near_index,
        tile_dst,
        inner_src,
        outer_src,
        tile_live,
        tile_weight,
    )
    return whitened, loss.reshape(())


def solution(mesh):
    placed = (
        P(("dom", "sub"), None),
        P(),
        P(("dom", "sub")),
        P(("dom", "sub")),
        P(("dom", "sub")),
        P(("dom", "sub")),
        P(("dom", "sub")),
        P(("dom", "sub"), None),
        P(("dom", "sub"), None, None),
    )
    return jax.shard_map(
        functools.partial(body, mesh.shape["dom"], mesh.shape["sub"]),
        mesh=mesh,
        in_specs=placed,
        out_specs=(P(("dom", "sub"), None), P()),
        check_vma=False,
    )
```

profile of v0, /device:TPU:0, one launch (start us, length us, event | category | flops | bytes accessed | tf_op | source)
XLA Modules:
  0.0 52.0 jit_solution(14589403341662787308)
XLA Ops:
  0.6 47.8 %shard_map.104 = (bf16[1024,256]{1,0:T(8,128)(2,1)}, f32[1,1]{1,0:T(1,128)}) custom-call(bf16[8,128,256]{2,1,0:T(8,128)(2,1)} %bitcast.4, bf16[256,256]{1,0:T(8,128)(2,1)} %weight_in.1, s32[1,512]{1,0:T(1,128)} %bitcast.5, s32[1,128]{1,0:T(1,128)} %bitcast.6, s32[16]{0:T(128)} %dst_in.1, s32[8]{0:T(128)} %inner_in.1, s32[8]{0:T(128)} %outer_in.1, ...), custom_call_target="tpu_custom_call" | custom-call | tf_op jit(solution)/shard_map/pallas_call | solution.py:456
  48.5 1.9 %copy.13 = bf16[1024,256]{1,0:T(8,128)(2,1)} copy(bf16[1024,256]{1,0:T(8,128)(2,1)} %get-tuple-element.8) | data formatting | bytes 1048576
where the time goes:
time: 52.2 us; the launch traced here: 52 us
  Pallas kernels  47.8 us (92%)
  between operations  2.34 us (4%)
  local copies, waits for them, and re-layouts  1.87 us (4%)
    pallas_call x1, Pallas kernels, body(): pl.pallas_call(functools.partial(kernel, n_dom, n_sub, near_count // n_su...  47.8 us
    unnamed x1, local copies, waits for them, and re-layouts  1.87 us

commit v1 on v0

--- a/solution.py
+++ b/solution.py
@@ -82,6 +82,19 @@
     return jnp.concatenate(done, axis=0)
 
 
+def far_first(index, count, turn):
+    if count % 2:
+        return lax.rem(index + 1 + turn, count)
+    half = count // 2
+    mine = lax.div(index, half) * half
+    other = half - mine
+    return jnp.where(
+        turn < half,
+        other + lax.rem(index + half // 2 + turn, half),
+        mine + lax.rem(index + 1 + turn, half),
+    )
+
+
 def kernel(
     n_dom,
     n_sub,
@@ -114,12 +127,11 @@
     products,
     acc,
     aggregate,
-    gram_part,
-    gram_in,
-    gram_own,
-    gram,
-    loss_own,
-    loss_all,
+    features_t,
+    part,
+    part_in,
+    part_own,
+    whole,
     work,
     load_sems,
     halo_sems,
@@ -132,16 +144,17 @@
     tiles, size, feat = features_ref.shape
     rows = tiles * size
     slots = inner_ref.shape[0]
-    share = gram_own.shape[0]
-    owners = gram_part.shape[0] // share
-    mine = lax.div(me * owners + total_devices - 1, total_devices)
-    owns = jnp.logical_and(mine < owners, lax.div(mine * total_devices, owners) == me)
-
-    def home(owner):
-        return lax.div(owner * total_devices, owners)
+    share = part_own.shape[1]
+    owners = part.shape[1] // share
+    first_owner = (total_devices - owners) // 2
+    mine = me - first_owner
+    owns = jnp.logical_and(mine >= 0, mine < owners)
 
     def share_rows(owner):
         return pl.ds(pl.multiple_of(owner * share, share), share)
+
+    def device_of(index):
+        return (lax.div(index, n_sub), lax.rem(index, n_sub))
 
     incoming = (
         (far_in, far_ref),
@@ -159,9 +172,6 @@
         for place, (source, target) in enumerate(incoming)
     ]
 
-    def device_of(index):
-        return (lax.div(index, n_sub), lax.rem(index, n_sub))
-
     barrier = pltpu.get_barrier_semaphore()
 
     @pl.loop(1, total_devices)
@@ -208,9 +218,9 @@
 
     pl.semaphore_wait(barrier, total_devices - 1)
 
-    @pl.loop(1, n_dom)
-    def _(offset):
-        peer = lax.rem(dom + offset, n_dom)
+    @pl.loop(0, n_dom - 1)
+    def _(turn):
+        peer = far_first(dom, n_dom, turn)
         pltpu.make_async_remote_copy(
             src_ref=far_send.at[dom_rows(peer)],
             dst_ref=dom_place(dom),
@@ -220,9 +230,9 @@
             device_id_type=MESH,
         ).start()
 
-    @pl.loop(1, n_sub)
-    def _(offset):
-        peer = lax.rem(sub + offset, n_sub)
+    @pl.loop(0, n_sub - 1)
+    def _(turn):
+        peer = far_first(sub, n_sub, turn)
         pltpu.make_async_remote_copy(
             src_ref=near_send.at[sub_rows(peer)],
             dst_ref=sub_place(sub),
@@ -255,6 +265,12 @@
     for load in loads[3:]:
         load.wait()
     slot_products(features_ref, inner_ref, 0)
+    features_t[...] = features.T
+    squares = features.astype(jnp.float32)
+    squares = jnp.sum(squares * squares, axis=0, keepdims=True)
+    square_row = squares[:, :128]
+    for side in range(128, feat, 128):
+        square_row = square_row + squares[:, side : side + 128]
     inner_count = jnp.full((1, feat), live_ref[0, 0], jnp.int32)
     outer_count = jnp.full((1, feat), live_ref[0, 1], jnp.int32)
 
@@ -285,70 +301,148 @@
         features_ref[...].reshape(rows, feat).astype(jnp.float32) + projected / (1.0 + jnp.exp(-projected))
     ).astype(jnp.bfloat16)
     hidden_t = hidden.T
-    blocks = [(top, side) for top in range(0, feat, 128) for side in range(top, feat, 128)]
-    for top in range(0, feat, 128):
+    row = lax.broadcasted_iota(jnp.int32, (128, 128), 0)
+    lane = lax.broadcasted_iota(jnp.int32, (128, 128), 1)
+    tops = range(0, feat, 256)
+    sides = [(top, side) for top in range(0, feat, 128) for side in range(top + 128, feat, 128)]
+    pair_at = {top: top // 2 for top in tops}
+    side_at = {pair: feat // 2 + 128 * place for place, pair in enumerate(sides)}
+    extra_at = feat // 2 + 128 * len(sides)
+
+    def diagonal_row(block):
+        return jnp.sum(jnp.where(row == lane, block, 0.0), axis=0, keepdims=True)
+
+    def send_parts(kind):
+        half = owners // 2
+        left = me < total_devices // 2
+        first_count = jnp.where(left, owners - half, half)
+        first_base = jnp.where(left, half, 0)
+        last_count = owners - first_count
+        last_base = half - first_base
+
+        @pl.loop(0, owners)
+        def _(turn):
+            owner = jnp.where(
+                turn < first_count,
+                first_base + lax.rem(me + turn, first_count),
+                last_base + lax.rem(me + turn, last_count),
+            )
+            peer = first_owner + owner
+
+            @pl.when(peer != me)
+            def _():
+                pltpu.make_async_remote_copy(
+                    src_ref=part.at[kind, share_rows(owner)],
+                    dst_ref=part_in.at[kind, me],
+                    send_sem=sum_sems.at[4 * kind],
+                    recv_sem=sum_sems.at[4 * kind + 1],
+                    device_id=device_of(peer),
+                    device_id_type=MESH,
+                ).start()
+
+    def share_sum(kind):
+        @pl.when(owns)
+        def _():
+            part_in[kind, me] = part[kind, share_rows(mine), :]
+            settle(part_in.at[kind, pl.ds(0, total_devices - 1)], sum_sems.at[4 * kind + 1])
+            total = jnp.sum(part_in[kind], axis=0)
+            part_own[kind] = total
+            whole[kind, share_rows(mine), :] = total
+
+            @pl.loop(0, total_devices - 1)
+            def _(turn):
+                peer = far_first(me, total_devices, turn)
+                pltpu.make_async_remote_copy(
+                    src_ref=part_own.at[kind],
+                    dst_ref=whole.at[kind, share_rows(mine)],
+                    send_sem=sum_sems.at[4 * kind + 2],
+                    recv_sem=sum_sems.at[4 * kind + 3],
+                    device_id=device_of(peer),
+                    device_id_type=MESH,
+                ).start()
+
+    def await_sum(kind):
+        @pl.when(owns)
+        def _():
+            settle(whole.at[kind, pl.ds(0, share * (owners - 1))], sum_sems.at[4 * kind + 3])
+
+        @pl.when(jnp.logical_not(owns))
+        def _():
+            settle(whole.at[kind], sum_sems.at[4 * kind + 3])
+
+    def await_sends(kind):
+        @pl.when(owns)
+        def _():
+            settle(part.at[kind, pl.ds(0, share * (owners - 1))], sum_sems.at[4 * kind])
+            settle(part_in.at[kind, pl.ds(0, total_devices - 1)], sum_sems.at[4 * kind + 2])
+
+        @pl.when(jnp.logical_not(owns))
+        def _():
+            settle(part.at[kind], sum_sems.at[4 * kind])
+
+    part[:, extra_at:, :] = jnp.zeros((2, part.shape[1] - extra_at, 128), jnp.float32)
+    stripes = {
+        top: jnp.dot(hidden_t[top : top + 128, :], hidden[:, top:], preferred_element_type=jnp.float32)
+        for top in range(0, feat, 128)
+    }
+    for top in tops:
+        low = stripes[top + 128][:, :128]
+        part[0, pair_at[top] : pair_at[top] + 128, :] = jnp.where(row <= lane, stripes[top][:, :128], low)
+        place = extra_at + top // 256
+        part[0, place : place + 1, :] = diagonal_row(low)
+    for top, side in sides:
+        at = side_at[top, side]
+        part[0, at : at + 128, :] = stripes[top][:, side - top : side - top + 128]
+    send_parts(0)
+
+    for top in tops:
         stripe = jnp.dot(
-            hidden_t[top : top + 128, :], hidden[:, top:], preferred_element_type=jnp.float32
+            features_t[top:, :], hidden[:, top : top + 128], preferred_element_type=jnp.float32
         )
-        for side in range(top, feat, 128):
-            at = 128 * blocks.index((top, side))
-            gram_part[at : at + 128, :] = stripe[:, side - top : side - top + 128]
-
-    @pl.loop(0, owners)
-    def _(turn):
-        owner = lax.rem(mine + turn, owners)
-        peer = home(owner)
-
-        @pl.when(peer != me)
-        def _():
-            pltpu.make_async_remote_copy(
-                src_ref=gram_part.at[share_rows(owner)],
-                dst_ref=gram_in.at[me],
-                send_sem=sum_sems.at[0],
-                recv_sem=sum_sems.at[1],
-                device_id=device_of(peer),
-                device_id_type=MESH,
-            ).start()
-
-    @pl.when(owns)
-    def _():
-        gram_in[me] = gram_part[share_rows(mine), :]
-        settle(gram_in.at[pl.ds(0, total_devices - 1)], sum_sems.at[1])
-        total = jnp.sum(gram_in[...], axis=0)
-        gram_own[...] = total
-        gram[share_rows(mine), :] = total
-
-        @pl.loop(1, total_devices)
-        def _(offset):
-            peer = lax.rem(me + offset, total_devices)
-            pltpu.make_async_remote_copy(
-                src_ref=gram_own,
-                dst_ref=gram.at[share_rows(mine)],
-                send_sem=sum_sems.at[2],
-                recv_sem=sum_sems.at[3],
-                device_id=device_of(peer),
-                device_id_type=MESH,
-            ).start()
-
-        settle(gram.at[pl.ds(0, share * (owners - 1))], sum_sems.at[3])
-
-    @pl.when(jnp.logical_not(owns))
-    def _():
-        settle(gram, sum_sems.at[3])
+        low = jnp.dot(
+            hidden_t[top + 128 : top + 256, :],
+            features_ref[...].reshape(rows, feat)[:, top + 128 : top + 256],
+            preferred_element_type=jnp.float32,
+        )
+        part[1, pair_at[top] : pair_at[top] + 128, :] = jnp.where(row >= lane, stripe[:128, :], low)
+        place = extra_at + top // 256
+        part[1, place : place + 1, :] = diagonal_row(low)
+        for side in range(top + 128, feat, 128):
+            at = side_at[top, side]
+            part[1, at : at + 128, :] = stripe[side - top : side - top + 128, :]
+    for top in range(128, feat, 256):
+        for side in range(top + 128, feat, 128):
+            at = side_at[top, side]
+            part[1, at : at + 128, :] = jnp.dot(
+                features_t[side : side + 128, :],
+                hidden[:, top : top + 128],
+                preferred_element_type=jnp.float32,
+            )
+    square_at = extra_at + feat // 256
+    part[1, square_at : square_at + 1, :] = square_row
+    send_parts(1)
+    share_sum(0)
+    share_sum(1)
+    await_sum(0)
 
     vertex_count = rows * total_devices
     diagonal = lax.broadcasted_iota(jnp.int32, (feat, feat), 0) == lax.broadcasted_iota(
         jnp.int32, (feat, feat), 1
     )
     identity = jnp.where(diagonal, 1.0, 0.0)
-    for top, side in blocks:
-        at = 128 * blocks.index((top, side))
-        work[top : top + 128, side : side + 128] = (
-            gram[at : at + 128, :] / vertex_count
-            + epsilon * identity[top : top + 128, side : side + 128]
-        )
-        if side > top:
-            work[side : side + 128, top : top + 128] = jnp.zeros((128, 128), jnp.float32)
+    inner_identity = epsilon * identity[:128, :128]
+    for top in tops:
+        pair = whole[0, pair_at[top] : pair_at[top] + 128, :] / vertex_count
+        turned = pair.T
+        place = extra_at + top // 256
+        low_diagonal = whole[0, place : place + 1, :] / vertex_count
+        work[top : top + 128, top : top + 128] = jnp.where(row <= lane, pair, turned) + inner_identity
+        low = jnp.where(row == lane, low_diagonal, jnp.where(row > lane, pair, turned))
+        work[top + 128 : top + 256, top + 128 : top + 256] = low + inner_identity
+    for top, side in sides:
+        at = side_at[top, side]
+        work[top : top + 128, side : side + 128] = whole[0, at : at + 128, :] / vertex_count
+        work[side : side + 128, top : top + 128] = jnp.zeros((128, 128), jnp.float32)
     work[:, feat:] = identity
     for start in range(0, feat, LEAF):
         stop = start + LEAF
@@ -377,41 +471,31 @@
     store = pltpu.make_async_copy(result, out_ref, load_sems.at[len(loads)])
     store.start()
 
-    distance = white - features_ref[...].reshape(rows, feat).astype(jnp.float32)
-    wide = jnp.sum(distance * distance, axis=0, keepdims=True)
-    partial = wide[:, :128]
-    for side in range(128, feat, 128):
-        partial = partial + wide[:, side : side + 128]
-    loss_own[...] = partial
-    loss_all[me] = partial
-
-    @pl.loop(1, total_devices)
-    def _(offset):
-        peer = lax.rem(me + offset, total_devices)
-        pltpu.make_async_remote_copy(
-            src_ref=loss_own,
-            dst_ref=loss_all.at[me],
-            send_sem=sum_sems.at[4],
-            recv_sem=sum_sems.at[5],
-            device_id=device_of(peer),
-            device_id_type=MESH,
-        ).start()
-
     settle(far_send.at[pl.ds(0, per_dom * (n_dom - 1))], halo_sems.at[0])
     settle(near_send.at[pl.ds(0, per_sub * (n_sub - 1))], halo_sems.at[2])
 
-    @pl.when(owns)
-    def _():
-        settle(gram_part.at[pl.ds(0, share * (owners - 1))], sum_sems.at[0])
-        settle(gram_in.at[pl.ds(0, total_devices - 1)], sum_sems.at[2])
-
-    @pl.when(jnp.logical_not(owns))
-    def _():
-        settle(gram_part, sum_sems.at[0])
-
-    settle(loss_all.at[pl.ds(0, total_devices - 1)], sum_sems.at[4])
-    settle(loss_all.at[pl.ds(0, total_devices - 1)], sum_sems.at[5])
-    loss_ref[0, 0] = jnp.sum(jnp.sum(loss_all[...], axis=0)) / (vertex_count * feat)
+    await_sends(0)
+    await_sends(1)
+    await_sum(1)
+    cross = jnp.zeros((128, 128), jnp.float32)
+    norm = jnp.zeros((128, 128), jnp.float32)
+    for top in tops:
+        upper = work[top : top + 128, feat + top : feat + top + 128]
+        lower = work[top + 128 : top + 256, feat + top + 128 : feat + top + 256]
+        place = extra_at + top // 256
+        pair = whole[1, pair_at[top] : pair_at[top] + 128, :]
+        low_diagonal = whole[1, place : place + 1, :]
+        cross = cross + jnp.where(row >= lane, upper, lower.T) * pair
+        cross = cross + jnp.where(row == lane, lower * low_diagonal, 0.0)
+        norm = norm + upper * upper + lower * lower
+    for top, side in sides:
+        at = side_at[top, side]
+        across_block = work[side : side + 128, feat + top : feat + top + 128]
+        cross = cross + across_block * whole[1, at : at + 128, :]
+        norm = norm + across_block * across_block
+    rest = jnp.sum(-2.0 * cross - (vertex_count * epsilon) * norm, axis=0, keepdims=True)
+    rest = rest + whole[1, square_at : square_at + 1, :]
+    loss_ref[0, 0] = 1.0 + jnp.sum(rest) / (vertex_count * feat)
     store.wait()
 
 
@@ -432,11 +516,13 @@
     size = tile_weight.shape[1]
     slots = inner_src.shape[0]
     total = n_dom * n_sub
-    tiles_wide = feat // 128
-    packed_rows = 128 * (tiles_wide * (tiles_wide + 1) // 2)
+    wide = feat // 128
+    extra = feat // 256 + 1
+    packed_rows = feat // 2 + 64 * wide * (wide - 1) + extra
     share = 8
-    while packed_rows % share or packed_rows // share > total:
+    while -(-packed_rows // share) > total // 2 + 1:
         share += 8
+    packed_rows = -(-packed_rows // share) * share
     far_count = send_far.shape[0]
     near_count = send_near.shape[0]
 
@@ -479,16 +565,15 @@
             pltpu.VMEM((slots, size, feat), f32),
             pltpu.VMEM((rows // size, size, feat), f32),
             pltpu.VMEM((rows, feat), bf16),
-            pltpu.VMEM((packed_rows, 128), f32),
-            pltpu.VMEM((total, share, 128), f32),
-            pltpu.VMEM((share, 128), f32),
-            pltpu.VMEM((packed_rows, 128), f32),
-            pltpu.VMEM((1, 128), f32),
-            pltpu.VMEM((total, 1, 128), f32),
+            pltpu.VMEM((feat, rows), bf16),
+            pltpu.VMEM((2, packed_rows, 128), f32),
+            pltpu.VMEM((2, total, share, 128), f32),
+            pltpu.VMEM((2, share, 128), f32),
+            pltpu.VMEM((2, packed_rows, 128), f32),
             pltpu.VMEM((feat, 2 * feat), f32),
             pltpu.SemaphoreType.DMA((10,)),
             pltpu.SemaphoreType.DMA((4,)),
-            pltpu.SemaphoreType.DMA((6,)),
+            pltpu.SemaphoreType.DMA((8,)),
         ],
         compiler_params=pltpu.CompilerParams(collective_id=0, has_side_effects=True),
     )(

time: 52.2 us -> 46.1 us (0.88)
  Pallas kernels: 47.8 us -> 41.7 us
    pallas_call x1, Pallas kernels: 47.8 us -> 41.7 us  [body(): pl.pallas_call(functools.partial(kernel, n_dom, n_sub, near_count // n_su...]
where the time goes in v1:
time: 46.1 us; the launch traced here: 45.9 us
  Pallas kernels  41.7 us (90%)
  between operations  2.34 us (5%)
  local copies, waits for them, and re-layouts  1.87 us (4%)
    pallas_call x1, Pallas kernels, body(): pl.pallas_call(functools.partial(kernel, n_dom, n_sub, near_count // n_su...  41.7 us
    unnamed x1, local copies, waits for them, and re-layouts  1.87 us

profile of v1, /device:TPU:0, one launch (start us, length us, event | category | flops | bytes accessed | tf_op | source)
XLA Modules:
  0.0 45.9 jit_solution(413568248488783873)
XLA Ops:
  0.6 41.7 %shard_map.104 = (bf16[1024,256]{1,0:T(8,128)(2,1)}, f32[1,1]{1,0:T(1,128)}) custom-call(bf16[8,128,256]{2,1,0:T(8,128)(2,1)} %bitcast.4, bf16[256,256]{1,0:T(8,128)(2,1)} %weight_in.1, s32[1,512]{1,0:T(1,128)} %bitcast.5, s32[1,128]{1,0:T(1,128)} %bitcast.6, s32[16]{0:T(128)} %dst_in.1, s32[8]{0:T(128)} %inner_in.1, s32[8]{0:T(128)} %outer_in.1, ...), custom_call_target="tpu_custom_call" | custom-call | tf_op jit(solution)/shard_map/pallas_call | solution.py:542
  42.3 1.9 %copy.13 = bf16[1024,256]{1,0:T(8,128)(2,1)} copy(bf16[1024,256]{1,0:T(8,128)(2,1)} %get-tuple-element.8) | data formatting | bytes 1048576

commit v2 on v1

--- a/solution.py
+++ b/solution.py
@@ -9,8 +9,8 @@
 
 epsilon = 1e-05
 MESH = pl.DeviceIdType.MESH
-LEAF = 64
-HIGH = lax.Precision.HIGHEST
+LEAF = 32
+GROUP = 16
 
 
 def one_hot_rows(index_row, row_count):
@@ -43,43 +43,75 @@
     return jnp.where(place == column, 1.0, 0.0).astype(jnp.bfloat16)
 
 
-def leaf_inverse(block):
-    size = block.shape[0]
-    row = lax.broadcasted_iota(jnp.int32, (size, size), 0)
-    lane = lax.broadcasted_iota(jnp.int32, (size, size), 1)
-    work = jnp.concatenate([block, jnp.where(row == lane, 1.0, 0.0)], axis=1)
-    group = 8
-    done = []
-    for step in range(0, size, group):
-        lines = [work[i : i + 1, :] for i in range(group)]
-        entry = {
-            (i, j): jnp.broadcast_to(lines[i][:, step + j : step + j + 1], (1, 2 * size))
-            for i in range(group)
-            for j in range(i, group)
-        }
-        inverse = []
-        for i in range(group):
-            inverse.append(1.0 / entry[i, i])
-            for j in range(i + 1, group):
-                share = entry[i, j] * inverse[i]
-                for k in range(j, group):
-                    entry[j, k] = entry[j, k] - share * entry[i, k]
-                lines[j] = lines[j] - share * lines[i]
-            done.append((lines[i] / jnp.sqrt(entry[i, i]))[:, size:])
-        if step + group == size:
-            break
-        solved = [None] * group
-        for i in reversed(range(group)):
-            line = lines[i]
-            for j in range(i + 1, group):
-                line = line - entry[i, j] * solved[j]
-            solved[i] = line * inverse[i]
-        work = work[group:, :]
-        update = work[:, step : step + 1] * solved[0]
-        for i in range(1, group):
-            update = update + work[:, step + i : step + i + 1] * solved[i]
-        work = work - update
-    return jnp.concatenate(done, axis=0)
+def thirds(block):
+    high = block.astype(jnp.bfloat16)
+    rest = block - high.astype(jnp.float32)
+    mid = rest.astype(jnp.bfloat16)
+    low = (rest - mid.astype(jnp.float32)).astype(jnp.bfloat16)
+    return high, mid, low
+
+
+def factor_rows(lines, lanes):
+    count = len(lines[0])
+    sub = lax.broadcasted_iota(jnp.int32, (8, 128), 0)
+    pivots = [jnp.zeros((8, 128), jnp.float32)] * count
+    for start in range(0, 8 * count, GROUP):
+        tall = range(start // 8, count)
+        columns = []
+        for k in range(start, start + GROUP):
+            tile, lane = divmod(lanes + k, 128)
+            columns.append({
+                v: jnp.broadcast_to(lines[tile][v][:, lane : lane + 1], (8, 128)) for v in tall
+            })
+        for i in range(GROUP):
+            home, place = divmod(start + i, 8)
+            pivot = jnp.broadcast_to(columns[i][home][place : place + 1, :], (8, 128))
+            pivots[home] = jnp.where(sub == place, pivot, pivots[home])
+            inverse = 1.0 / pivot
+            below = range(home, count)
+            factor = {v: columns[i][v] * inverse for v in below}
+            for k in range(i + 1, GROUP):
+                entry = jnp.broadcast_to(columns[k][home][place : place + 1, :], (8, 128))
+                for v in below:
+                    columns[k][v] = columns[k][v] - factor[v] * entry
+            factor[home] = jnp.where(sub > place, factor[home], 0.0)
+            for tile in lines:
+                entry = jnp.broadcast_to(tile[home][place : place + 1, :], (8, 128))
+                for v in below:
+                    tile[v] = tile[v] - factor[v] * entry
+    scale = [lax.rsqrt(pivot) for pivot in pivots]
+    return [
+        jnp.concatenate([line * by for line, by in zip(tile, scale)], axis=0) for tile in lines
+    ]
+
+
+def factor_inverse(work, feat):
+    count = LEAF // 8
+    for start in range(0, feat, LEAF):
+        stop = start + LEAF
+        first = start // 128
+        tiles = list(range(first, feat // 128 + (stop - 1) // 128 + 1))
+        lines = [
+            [work[start + 8 * v : start + 8 * v + 8, 128 * t : 128 * t + 128] for v in range(count)]
+            for t in tiles
+        ]
+        done = jnp.concatenate(factor_rows(lines, start - 128 * first), axis=1)
+        work[start:stop, 128 * first : 128 * (tiles[-1] + 1)] = done
+        if stop < feat:
+            high, mid, low = thirds(done)
+            left = jnp.concatenate([high, high, mid, high, mid, low], axis=0)
+            right = jnp.concatenate([high, mid, high, low, mid, high], axis=0)
+            span = slice(128 * (stop // 128), 128 * (tiles[-1] + 1))
+            skip = span.start - 128 * first
+            for top, bottom in ((stop, stop + LEAF), (stop + LEAF, feat)):
+                if top < bottom:
+                    update = lax.dot_general(
+                        left[:, top - 128 * first : bottom - 128 * first],
+                        right[:, skip:],
+                        (((0,), (0,)), ((), ())),
+                        preferred_element_type=jnp.float32,
+                    )
+                    work[top:bottom, span] = work[top:bottom, span] - update
 
 
 def far_first(index, count, turn):
@@ -444,21 +476,7 @@
         work[top : top + 128, side : side + 128] = whole[0, at : at + 128, :] / vertex_count
         work[side : side + 128, top : top + 128] = jnp.zeros((128, 128), jnp.float32)
     work[:, feat:] = identity
-    for start in range(0, feat, LEAF):
-        stop = start + LEAF
-        inverse = leaf_inverse(work[start:stop, start:stop])
-        pivot_rows = jnp.dot(
-            inverse, work[start:stop, :], precision=HIGH, preferred_element_type=jnp.float32
-        )
-        work[start:stop, :] = pivot_rows
-        if stop < feat:
-            work[stop:, :] = work[stop:, :] - lax.dot_general(
-                pivot_rows[:, stop:feat],
-                pivot_rows,
-                (((0,), (0,)), ((), ())),
-                precision=HIGH,
-                preferred_element_type=jnp.float32,
-            )
+    factor_inverse(work, feat)
 
     lower_inverse = work[:, feat:]
     high_part = lower_inverse.astype(jnp.bfloat16)

time: 46.1 us -> 40.9 us (0.89)
  Pallas kernels: 41.7 us -> 36.5 us
    pallas_call x1, Pallas kernels: 41.7 us -> 36.5 us  [body(): pl.pallas_call(functools.partial(kernel, n_dom, n_sub, near_count // n_su...]
where the time goes in v2:
time: 40.9 us; the launch traced here: 40.7 us
  Pallas kernels  36.5 us (89%)
  between operations  2.34 us (6%)
  local copies, waits for them, and re-layouts  1.87 us (5%)
    pallas_call x1, Pallas kernels, body(): pl.pallas_call(functools.partial(kernel, n_dom, n_sub, near_count // n_su...  36.5 us
    unnamed x1, local copies, waits for them, and re-layouts  1.87 us

profile of v2, /device:TPU:0, one launch (start us, length us, event | category | flops | bytes accessed | tf_op | source)
XLA Modules:
  0.0 40.7 jit_solution(3675787364253860433)
XLA Ops:
  0.6 36.5 %shard_map.104 = (bf16[1024,256]{1,0:T(8,128)(2,1)}, f32[1,1]{1,0:T(1,128)}) custom-call(bf16[8,128,256]{2,1,0:T(8,128)(2,1)} %bitcast.4, bf16[256,256]{1,0:T(8,128)(2,1)} %weight_in.1, s32[1,512]{1,0:T(1,128)} %bitcast.5, s32[1,128]{1,0:T(1,128)} %bitcast.6, s32[16]{0:T(128)} %dst_in.1, s32[8]{0:T(128)} %inner_in.1, s32[8]{0:T(128)} %outer_in.1, ...), custom_call_target="tpu_custom_call" | custom-call | tf_op jit(solution)/shard_map/pallas_call | solution.py:560
  37.1 1.9 %copy.13 = bf16[1024,256]{1,0:T(8,128)(2,1)} copy(bf16[1024,256]{1,0:T(8,128)(2,1)} %get-tuple-element.8) | data formatting | bytes 1048576

commit v3 on v2

--- a/solution.py
+++ b/solution.py
@@ -11,6 +11,8 @@
 MESH = pl.DeviceIdType.MESH
 LEAF = 32
 GROUP = 16
+CHUNKS = 4
+VMEM_LIMIT = 32 * 1024 * 1024
 
 
 def one_hot_rows(index_row, row_count):
@@ -140,7 +142,8 @@
     outer_in,
     live_in,
     tile_in,
-    out_ref,
+    hidden_ref,
+    inverse_ref,
     loss_ref,
     features_ref,
     weight_ref,
@@ -151,7 +154,6 @@
     outer_ref,
     live_ref,
     tile_ref,
-    result,
     far_send,
     near_send,
     arrived,
@@ -332,6 +334,7 @@
     hidden = (
         features_ref[...].reshape(rows, feat).astype(jnp.float32) + projected / (1.0 + jnp.exp(-projected))
     ).astype(jnp.bfloat16)
+    hidden_ref[...] = hidden
     hidden_t = hidden.T
     row = lax.broadcasted_iota(jnp.int32, (128, 128), 0)
     lane = lax.broadcasted_iota(jnp.int32, (128, 128), 1)
@@ -481,13 +484,8 @@
     lower_inverse = work[:, feat:]
     high_part = lower_inverse.astype(jnp.bfloat16)
     low_part = (lower_inverse - high_part.astype(jnp.float32)).astype(jnp.bfloat16)
-    across = (((1,), (1,)), ((), ()))
-    white = lax.dot_general(
-        hidden, high_part, across, preferred_element_type=jnp.float32
-    ) + lax.dot_general(hidden, low_part, across, preferred_element_type=jnp.float32)
-    result[...] = white.astype(jnp.bfloat16)
-    store = pltpu.make_async_copy(result, out_ref, load_sems.at[len(loads)])
-    store.start()
+    inverse_ref[0] = high_part
+    inverse_ref[1] = low_part
 
     settle(far_send.at[pl.ds(0, per_dom * (n_dom - 1))], halo_sems.at[0])
     settle(near_send.at[pl.ds(0, per_sub * (n_sub - 1))], halo_sems.at[2])
@@ -514,7 +512,26 @@
     rest = jnp.sum(-2.0 * cross - (vertex_count * epsilon) * norm, axis=0, keepdims=True)
     rest = rest + whole[1, square_at : square_at + 1, :]
     loss_ref[0, 0] = 1.0 + jnp.sum(rest) / (vertex_count * feat)
-    store.wait()
+
+
+def whiten(hidden_ref, inverse_ref, loss_in, out_ref, loss_ref, result, sems):
+    rows = hidden_ref.shape[0]
+    across = (((1,), (1,)), ((), ()))
+    step = rows // CHUNKS
+    stores = []
+    for chunk in range(CHUNKS):
+        here = pl.ds(chunk * step, step)
+        hidden = hidden_ref[here, :]
+        white = lax.dot_general(
+            hidden, inverse_ref[0], across, preferred_element_type=jnp.float32
+        ) + lax.dot_general(hidden, inverse_ref[1], across, preferred_element_type=jnp.float32)
+        result[here, :] = white.astype(jnp.bfloat16)
+        store = pltpu.make_async_copy(result.at[here], out_ref.at[here], sems.at[chunk])
+        store.start()
+        stores.append(store)
+    loss_ref[0, 0] = loss_in[0, 0]
+    for store in stores:
+        store.wait()
 
 
 def body(
@@ -553,18 +570,20 @@
     near_index = padded(send_near, n_sub)
     far_padded = far_index.shape[1]
     near_padded = near_index.shape[1]
-    anywhere = pl.BlockSpec(memory_space=pl.ANY)
+    anywhere = pl.BlockSpec(memory_space=pltpu.HBM)
     smem = pl.BlockSpec(memory_space=pltpu.SMEM)
     f32 = jnp.float32
     bf16 = jnp.bfloat16
-    whitened, loss = pl.pallas_call(
+    vmem = pl.BlockSpec(memory_space=pltpu.VMEM)
+    hidden, inverse, loss = pl.pallas_call(
         functools.partial(kernel, n_dom, n_sub, near_count // n_sub),
         out_shape=(
-            jax.ShapeDtypeStruct((rows, feat), bf16),
+            pltpu.VMEM((rows, feat), bf16),
+            pltpu.VMEM((2, feat, feat), bf16),
             jax.ShapeDtypeStruct((1, 1), f32),
         ),
         in_specs=[anywhere] * 9,
-        out_specs=(anywhere, smem),
+        out_specs=(vmem, vmem, smem),
         scratch_shapes=[
             pltpu.VMEM((rows // size, size, feat), bf16),
             pltpu.VMEM(weight.shape, bf16),
@@ -575,7 +594,6 @@
             pltpu.SMEM(outer_src.shape, jnp.int32),
             pltpu.SMEM(tile_live.shape, jnp.int32),
             pltpu.VMEM(tile_weight.shape, bf16),
-            pltpu.VMEM((rows, feat), bf16),
             pltpu.VMEM((far_padded, feat), bf16),
             pltpu.VMEM((near_padded, feat), bf16),
             pltpu.VMEM((far_padded + near_padded, feat), bf16),
@@ -593,18 +611,36 @@
             pltpu.SemaphoreType.DMA((4,)),
             pltpu.SemaphoreType.DMA((8,)),
         ],
-        compiler_params=pltpu.CompilerParams(collective_id=0, has_side_effects=True),
+        compiler_params=pltpu.CompilerParams(
+            collective_id=0, has_side_effects=True, vmem_limit_bytes=VMEM_LIMIT
+        ),
     )(
-        features.reshape(rows // size, size, feat),
-        weight,
-        far_index,
-        near_index,
-        tile_dst,
-        inner_src,
-        outer_src,
-        tile_live,
-        tile_weight,
+        *[
+            pltpu.with_memory_space_constraint(value, pltpu.HBM)
+            for value in (
+                features.reshape(rows // size, size, feat),
+                weight,
+                far_index,
+                near_index,
+                tile_dst,
+                inner_src,
+                outer_src,
+                tile_live,
+                tile_weight,
+            )
+        ]
     )
+    whitened, loss = pl.pallas_call(
+        whiten,
+        out_shape=(
+            jax.ShapeDtypeStruct((rows, feat), bf16),
+            jax.ShapeDtypeStruct((1, 1), f32),
+        ),
+        in_specs=[vmem, vmem, smem],
+        out_specs=(anywhere, smem),
+        scratch_shapes=[pltpu.VMEM((rows, feat), bf16), pltpu.SemaphoreType.DMA((CHUNKS,))],
+        compiler_params=pltpu.CompilerParams(vmem_limit_bytes=VMEM_LIMIT),
+    )(hidden, inverse, loss)
     return whitened, loss.reshape(())
 
 

time: 40.9 us -> 38.5 us (0.941)
  local copies, waits for them, and re-layouts: 1.87 us -> 0 us
  between operations: 2.34 us -> 0.64 us
  Pallas kernels: 36.5 us -> 37.7 us
    pallas_call x0 -> x1, Pallas kernels: none -> 2.35 us  [body(): pl.pallas_call(whiten, out_shape=(jax.ShapeDtypeStruct((rows, feat), bf16...]
    unnamed x1 -> x0, local copies, waits for them, and re-layouts: 1.87 us -> none
    pallas_call x1, Pallas kernels: 36.5 us -> 35.3 us  [body(): pl.pallas_call(functools.partial(kernel, n_dom, n_sub, near_count // n_su...]
where the time goes in v3:
time: 38.5 us; the launch traced here: 38.3 us
  Pallas kernels  37.7 us (98%)
  between operations  0.64 us (2%)
    pallas_call x1, Pallas kernels, body(): pl.pallas_call(functools.partial(kernel, n_dom, n_sub, near_count // n_su...  35.3 us
    pallas_call x1, Pallas kernels, body(): pl.pallas_call(whiten, out_shape=(jax.ShapeDtypeStruct((rows, feat), bf16...  2.35 us

profile of v3, /device:TPU:0, one launch (start us, length us, event | category | flops | bytes accessed | tf_op | source)
XLA Modules:
  0.0 38.3 jit_solution(16513078065221921536)
XLA Ops:
  0.6 35.3 %shard_map.104 = (bf16[1024,256]{1,0:T(8,128)(2,1)S(1)}, bf16[2,256,256]{2,1,0:T(8,128)(2,1)S(1)}, f32[1,1]{1,0:T(1,128)}) custom-call(bf16[8,128,256]{2,1,0:T(8,128)(2,1)} %bitcast.4, bf16[256,256]{1,0:T(8,128)(2,1)} %weight_in.1, s32[1,512]{1,0:T(1,128)} %bitcast.5, s32[1,128]{1,0:T(1,128)} %bitcast.6, s32[16]{0:T(128)} %dst_in.1, s32[8]{0:T(128)} %inner_in.1, ...), custom_call_target="tpu_custom_call" | custom-call | tf_op jit(solution)/shard_map/pallas_call | solution.py:578
  36.0 2.4 %shard_map.105 = (bf16[1024,256]{1,0:T(8,128)(2,1)}, f32[1,1]{1,0:T(1,128)}) custom-call(bf16[1024,256]{1,0:T(8,128)(2,1)S(1)} %get-tuple-element.7.hidden_ref, bf16[2,256,256]{2,1,0:T(8,128)(2,1)S(1)} %get-tuple-element.8.inverse_ref, f32[1,1]{1,0:T(1,128)} %get-tuple-element.9.loss_in), custom_call_target="tpu_custom_call" | custom-call | tf_op jit(solution)/shard_map/pallas_call | solution.py:633

commit v4 on v3

--- a/solution.py
+++ b/solution.py
@@ -116,6 +116,14 @@
                     work[top:bottom, span] = work[top:bottom, span] - update
 
 
+def layout(feat):
+    tops = range(0, feat, 256)
+    sides = [(top, side) for top in range(0, feat, 128) for side in range(top + 128, feat, 128)]
+    pair_at = {top: top // 2 for top in tops}
+    side_at = {pair: feat // 2 + 128 * place for place, pair in enumerate(sides)}
+    return tops, sides, pair_at, side_at, feat // 2 + 128 * len(sides)
+
+
 def far_first(index, count, turn):
     if count % 2:
         return lax.rem(index + 1 + turn, count)
@@ -127,6 +135,18 @@
         other + lax.rem(index + half // 2 + turn, half),
         mine + lax.rem(index + 1 + turn, half),
     )
+
+
+def ends_first(index, count, turn, shift=0):
+    if count % 4:
+        return far_first(index, count, turn)
+    half = count // 2
+    block = count // 4
+    mine = lax.div(index, half) * half
+    step = lax.div(turn, block)
+    end = jnp.where(index < half, 3 - step, step) * block
+    across = end + lax.rem(index + shift + turn, block)
+    return jnp.where(turn < half, across, mine + lax.rem(index + 1 + turn, half))
 
 
 def kernel(
@@ -144,7 +164,7 @@
     tile_in,
     hidden_ref,
     inverse_ref,
-    loss_ref,
+    sums_ref,
     features_ref,
     weight_ref,
     far_ref,
@@ -208,25 +228,40 @@
 
     barrier = pltpu.get_barrier_semaphore()
 
-    @pl.loop(1, total_devices)
+    for load in loads[:3]:
+        load.start()
+
+    @pl.loop(1, n_dom)
     def _(offset):
-        peer = lax.rem(me + offset, total_devices)
-        pl.semaphore_signal(barrier, inc=1, device_id=device_of(peer), device_id_type=MESH)
-
-    for load in loads:
+        peer = lax.rem(dom + offset, n_dom)
+        pl.semaphore_signal(barrier, inc=1, device_id=(peer, sub), device_id_type=MESH)
+
+    @pl.loop(1, n_sub)
+    def _(offset):
+        peer = lax.rem(sub + offset, n_sub)
+        pl.semaphore_signal(barrier, inc=1, device_id=(dom, peer), device_id_type=MESH)
+
+    for load in loads[3:]:
         load.start()
     for load in loads[:3]:
         load.wait()
 
     features = features_ref[...].reshape(rows, feat)
-    far_rows = jnp.dot(
-        one_hot_rows(far_ref[...], rows), features, preferred_element_type=jnp.float32
-    ).astype(jnp.bfloat16)
-    near_rows = jnp.dot(
-        one_hot_rows(near_ref[...], rows), features, preferred_element_type=jnp.float32
-    ).astype(jnp.bfloat16)
-    far_send[...] = far_rows
-    near_send[...] = near_rows
+
+    def gather(index_row):
+        return jnp.dot(
+            one_hot_rows(index_row, rows), features, preferred_element_type=jnp.float32
+        ).astype(jnp.bfloat16)
+
+    far_half = far_send.shape[0] // 2
+    halved = n_dom % 4 == 0 and far_half % 128 == 0
+    across_first = pl.multiple_of(jnp.where(dom < n_dom // 2, far_half, 0), far_half)
+    inside_first = pl.multiple_of(far_half - across_first, far_half)
+    if halved:
+        far_send[pl.ds(across_first, far_half), :] = gather(far_ref[:, pl.ds(across_first, far_half)])
+    else:
+        far_send[...] = gather(far_ref[...])
+        near_send[...] = gather(near_ref[...])
     per_dom = far_send.shape[0] // n_dom
     per_sub = near_send.shape[0] // n_sub
     far_count = per_dom * n_dom
@@ -250,11 +285,10 @@
     def sub_place(index):
         return place(far_count + index * per_sub, per_sub)
 
-    pl.semaphore_wait(barrier, total_devices - 1)
-
-    @pl.loop(0, n_dom - 1)
-    def _(turn):
-        peer = far_first(dom, n_dom, turn)
+    pl.semaphore_wait(barrier, n_dom + n_sub - 2)
+
+    def send_far(turn):
+        peer = ends_first(dom, n_dom, turn, 0)
         pltpu.make_async_remote_copy(
             src_ref=far_send.at[dom_rows(peer)],
             dst_ref=dom_place(dom),
@@ -263,6 +297,14 @@
             device_id=(peer, sub),
             device_id_type=MESH,
         ).start()
+
+    if halved:
+        pl.loop(0, n_dom // 2)(send_far)
+        far_send[pl.ds(inside_first, far_half), :] = gather(far_ref[:, pl.ds(inside_first, far_half)])
+        pl.loop(n_dom // 2, n_dom - 1)(send_far)
+        near_send[...] = gather(near_ref[...])
+    else:
+        pl.loop(0, n_dom - 1)(send_far)
 
     @pl.loop(0, n_sub - 1)
     def _(turn):
@@ -338,11 +380,7 @@
     hidden_t = hidden.T
     row = lax.broadcasted_iota(jnp.int32, (128, 128), 0)
     lane = lax.broadcasted_iota(jnp.int32, (128, 128), 1)
-    tops = range(0, feat, 256)
-    sides = [(top, side) for top in range(0, feat, 128) for side in range(top + 128, feat, 128)]
-    pair_at = {top: top // 2 for top in tops}
-    side_at = {pair: feat // 2 + 128 * place for place, pair in enumerate(sides)}
-    extra_at = feat // 2 + 128 * len(sides)
+    tops, sides, pair_at, side_at, extra_at = layout(feat)
 
     def diagonal_row(block):
         return jnp.sum(jnp.where(row == lane, block, 0.0), axis=0, keepdims=True)
@@ -481,11 +519,7 @@
     work[:, feat:] = identity
     factor_inverse(work, feat)
 
-    lower_inverse = work[:, feat:]
-    high_part = lower_inverse.astype(jnp.bfloat16)
-    low_part = (lower_inverse - high_part.astype(jnp.float32)).astype(jnp.bfloat16)
-    inverse_ref[0] = high_part
-    inverse_ref[1] = low_part
+    inverse_ref[...] = work[:, feat:]
 
     settle(far_send.at[pl.ds(0, per_dom * (n_dom - 1))], halo_sems.at[0])
     settle(near_send.at[pl.ds(0, per_sub * (n_sub - 1))], halo_sems.at[2])
@@ -493,43 +527,51 @@
     await_sends(0)
     await_sends(1)
     await_sum(1)
+    sums_ref[...] = whole[1]
+
+
+def whiten(vertex_count, hidden_ref, inverse_ref, sums_ref, out_ref, loss_ref, result, sems):
+    rows = hidden_ref.shape[0]
+    across = (((1,), (1,)), ((), ()))
+    step = rows // CHUNKS
+    stores = []
+    inverse = inverse_ref[...]
+    high_part = inverse.astype(jnp.bfloat16)
+    low_part = (inverse - high_part.astype(jnp.float32)).astype(jnp.bfloat16)
+    for chunk in range(CHUNKS):
+        here = pl.ds(chunk * step, step)
+        hidden = hidden_ref[here, :]
+        white = lax.dot_general(
+            hidden, high_part, across, preferred_element_type=jnp.float32
+        ) + lax.dot_general(hidden, low_part, across, preferred_element_type=jnp.float32)
+        result[here, :] = white.astype(jnp.bfloat16)
+        store = pltpu.make_async_copy(result.at[here], out_ref.at[here], sems.at[chunk])
+        store.start()
+        stores.append(store)
+    feat = hidden_ref.shape[1]
+    tops, sides, pair_at, side_at, extra_at = layout(feat)
+    squares = extra_at + feat // 256
+    row = lax.broadcasted_iota(jnp.int32, (128, 128), 0)
+    lane = lax.broadcasted_iota(jnp.int32, (128, 128), 1)
     cross = jnp.zeros((128, 128), jnp.float32)
     norm = jnp.zeros((128, 128), jnp.float32)
     for top in tops:
-        upper = work[top : top + 128, feat + top : feat + top + 128]
-        lower = work[top + 128 : top + 256, feat + top + 128 : feat + top + 256]
+        upper = inverse_ref[top : top + 128, top : top + 128]
+        lower = inverse_ref[top + 128 : top + 256, top + 128 : top + 256]
         place = extra_at + top // 256
-        pair = whole[1, pair_at[top] : pair_at[top] + 128, :]
-        low_diagonal = whole[1, place : place + 1, :]
+        pair = sums_ref[pair_at[top] : pair_at[top] + 128, :]
+        low_diagonal = sums_ref[place : place + 1, :]
         cross = cross + jnp.where(row >= lane, upper, lower.T) * pair
         cross = cross + jnp.where(row == lane, lower * low_diagonal, 0.0)
         norm = norm + upper * upper + lower * lower
     for top, side in sides:
         at = side_at[top, side]
-        across_block = work[side : side + 128, feat + top : feat + top + 128]
-        cross = cross + across_block * whole[1, at : at + 128, :]
+        across_block = inverse_ref[side : side + 128, top : top + 128]
+        cross = cross + across_block * sums_ref[at : at + 128, :]
         norm = norm + across_block * across_block
     rest = jnp.sum(-2.0 * cross - (vertex_count * epsilon) * norm, axis=0, keepdims=True)
-    rest = rest + whole[1, square_at : square_at + 1, :]
+    rest = rest + sums_ref[squares : squares + 1, :]
     loss_ref[0, 0] = 1.0 + jnp.sum(rest) / (vertex_count * feat)
-
-
-def whiten(hidden_ref, inverse_ref, loss_in, out_ref, loss_ref, result, sems):
-    rows = hidden_ref.shape[0]
-    across = (((1,), (1,)), ((), ()))
-    step = rows // CHUNKS
-    stores = []
-    for chunk in range(CHUNKS):
-        here = pl.ds(chunk * step, step)
-        hidden = hidden_ref[here, :]
-        white = lax.dot_general(
-            hidden, inverse_ref[0], across, preferred_element_type=jnp.float32
-        ) + lax.dot_general(hidden, inverse_ref[1], across, preferred_element_type=jnp.float32)
-        result[here, :] = white.astype(jnp.bfloat16)
-        store = pltpu.make_async_copy(result.at[here], out_ref.at[here], sems.at[chunk])
-        store.start()
-        stores.append(store)
-    loss_ref[0, 0] = loss_in[0, 0]
     for store in stores:
         store.wait()
 
@@ -575,15 +617,15 @@
     f32 = jnp.float32
     bf16 = jnp.bfloat16
     vmem = pl.BlockSpec(memory_space=pltpu.VMEM)
-    hidden, inverse, loss = pl.pallas_call(
+    hidden, inverse, sums = pl.pallas_call(
         functools.partial(kernel, n_dom, n_sub, near_count // n_sub),
         out_shape=(
             pltpu.VMEM((rows, feat), bf16),
-            pltpu.VMEM((2, feat, feat), bf16),
-            jax.ShapeDtypeStruct((1, 1), f32),
+            pltpu.VMEM((feat, feat), f32),
+            pltpu.VMEM((packed_rows, 128), f32),
         ),
         in_specs=[anywhere] * 9,
-        out_specs=(vmem, vmem, smem),
+        out_specs=(vmem, vmem, vmem),
         scratch_shapes=[
             pltpu.VMEM((rows // size, size, feat), bf16),
             pltpu.VMEM(weight.shape, bf16),
@@ -631,16 +673,16 @@
         ]
     )
     whitened, loss = pl.pallas_call(
-        whiten,
+        functools.partial(whiten, rows * total),
         out_shape=(
             jax.ShapeDtypeStruct((rows, feat), bf16),
             jax.ShapeDtypeStruct((1, 1), f32),
         ),
-        in_specs=[vmem, vmem, smem],
+        in_specs=[vmem, vmem, vmem],
         out_specs=(anywhere, smem),
         scratch_shapes=[pltpu.VMEM((rows, feat), bf16), pltpu.SemaphoreType.DMA((CHUNKS,))],
         compiler_params=pltpu.CompilerParams(vmem_limit_bytes=VMEM_LIMIT),
-    )(hidden, inverse, loss)
+    )(hidden, inverse, sums)
     return whitened, loss.reshape(())
 
 

time: 38.5 us -> 35.2 us (0.914)
  Pallas kernels: 37.7 us -> 34.4 us
    pallas_call x1, Pallas kernels: 35.3 us -> 32.6 us  [body(): pl.pallas_call(functools.partial(kernel, n_dom, n_sub, near_count // n_su...]
    pallas_call x1, Pallas kernels: 2.35 us -> 1.73 us  [body(): pl.pallas_call(functools.partial(whiten, rows * total), out_shape=(jax.Sh...]
where the time goes in v4:
time: 35.2 us; the launch traced here: 35 us
  Pallas kernels  34.4 us (98%)
  between operations  0.64 us (2%)
    pallas_call x1, Pallas kernels, body(): pl.pallas_call(functools.partial(kernel, n_dom, n_sub, near_count // n_su...  32.6 us
    pallas_call x1, Pallas kernels, body(): pl.pallas_call(functools.partial(whiten, rows * total), out_shape=(jax.Sh...  1.73 us

profile of v4, /device:TPU:0, one launch (start us, length us, event | category | flops | bytes accessed | tf_op | source)
XLA Modules:
  0.0 35.0 jit_solution(803113806267584506)
XLA Ops:
  0.6 32.6 %shard_map.104 = (bf16[1024,256]{1,0:T(8,128)(2,1)S(1)}, f32[256,256]{1,0:T(8,128)S(1)}, f32[272,128]{1,0:T(8,128)S(1)}) custom-call(bf16[8,128,256]{2,1,0:T(8,128)(2,1)} %bitcast.4, bf16[256,256]{1,0:T(8,128)(2,1)} %weight_in.1, s32[1,512]{1,0:T(1,128)} %bitcast.5, s32[1,128]{1,0:T(1,128)} %bitcast.6, s32[16]{0:T(128)} %dst_in.1, s32[8]{0:T(128)} %inner_in.1, ...), custom_call_target="tpu_custom_call" | custom-call | tf_op jit(solution)/shard_map/pallas_call | solution.py:620
  33.3 1.7 %shard_map.105 = (bf16[1024,256]{1,0:T(8,128)(2,1)}, f32[1,1]{1,0:T(1,128)}) custom-call(bf16[1024,256]{1,0:T(8,128)(2,1)S(1)} %get-tuple-element.7.hidden_ref, f32[256,256]{1,0:T(8,128)S(1)} %get-tuple-element.8.inverse_ref, f32[272,128]{1,0:T(8,128)S(1)} %get-tuple-element.9.sums_ref), custom_call_target="tpu_custom_call" | custom-call | tf_op jit(solution)/shard_map/pallas_call | solution.py:675

commit v5 on v4

--- a/solution.py
+++ b/solution.py
@@ -12,6 +12,7 @@
 LEAF = 32
 GROUP = 16
 CHUNKS = 4
+UNROLL = 8
 VMEM_LIMIT = 32 * 1024 * 1024
 
 
@@ -87,9 +88,11 @@
     ]
 
 
-def factor_inverse(work, feat):
+def factor_inverse(work, feat, between):
     count = LEAF // 8
     for start in range(0, feat, LEAF):
+        if start == LEAF:
+            between()
         stop = start + LEAF
         first = start // 128
         tiles = list(range(first, feat // 128 + (stop - 1) // 128 + 1))
@@ -122,6 +125,21 @@
     pair_at = {top: top // 2 for top in tops}
     side_at = {pair: feat // 2 + 128 * place for place, pair in enumerate(sides)}
     return tops, sides, pair_at, side_at, feat // 2 + 128 * len(sides)
+
+
+def each(count, step):
+    whole, rest = divmod(count, UNROLL)
+    if whole > 1:
+
+        @pl.loop(0, whole)
+        def _(turn):
+            for place in range(UNROLL):
+                step(turn * UNROLL + place)
+    elif whole:
+        rest = count
+        whole = 0
+    for place in range(rest):
+        step(whole * UNROLL + place)
 
 
 def far_first(index, count, turn):
@@ -243,25 +261,25 @@
 
     for load in loads[3:]:
         load.start()
-    for load in loads[:3]:
-        load.wait()
-
-    features = features_ref[...].reshape(rows, feat)
-
-    def gather(index_row):
-        return jnp.dot(
-            one_hot_rows(index_row, rows), features, preferred_element_type=jnp.float32
-        ).astype(jnp.bfloat16)
-
+    loads[0].wait()
+    loads[1].wait()
     far_half = far_send.shape[0] // 2
     halved = n_dom % 4 == 0 and far_half % 128 == 0
     across_first = pl.multiple_of(jnp.where(dom < n_dom // 2, far_half, 0), far_half)
     inside_first = pl.multiple_of(far_half - across_first, far_half)
     if halved:
-        far_send[pl.ds(across_first, far_half), :] = gather(far_ref[:, pl.ds(across_first, far_half)])
+        across_picks = one_hot_rows(far_ref[:, pl.ds(across_first, far_half)], rows)
+    loads[2].wait()
+    features = features_ref[...].reshape(rows, feat)
+
+    def gather(picks):
+        return jnp.dot(picks, features, preferred_element_type=jnp.float32).astype(jnp.bfloat16)
+
+    if halved:
+        far_send[pl.ds(across_first, far_half), :] = gather(across_picks)
     else:
-        far_send[...] = gather(far_ref[...])
-        near_send[...] = gather(near_ref[...])
+        far_send[...] = gather(one_hot_rows(far_ref[...], rows))
+        near_send[...] = gather(one_hot_rows(near_ref[...], rows))
     per_dom = far_send.shape[0] // n_dom
     per_sub = near_send.shape[0] // n_sub
     far_count = per_dom * n_dom
@@ -299,10 +317,10 @@
         ).start()
 
     if halved:
-        pl.loop(0, n_dom // 2)(send_far)
-        far_send[pl.ds(inside_first, far_half), :] = gather(far_ref[:, pl.ds(inside_first, far_half)])
+        each(n_dom // 2, send_far)
+        far_send[pl.ds(inside_first, far_half), :] = gather(one_hot_rows(far_ref[:, pl.ds(inside_first, far_half)], rows))
         pl.loop(n_dom // 2, n_dom - 1)(send_far)
-        near_send[...] = gather(near_ref[...])
+        near_send[...] = gather(one_hot_rows(near_ref[...], rows))
     else:
         pl.loop(0, n_dom - 1)(send_far)
 
@@ -393,8 +411,7 @@
         last_count = owners - first_count
         last_base = half - first_base
 
-        @pl.loop(0, owners)
-        def _(turn):
+        def send(turn):
             owner = jnp.where(
                 turn < first_count,
                 first_base + lax.rem(me + turn, first_count),
@@ -413,6 +430,8 @@
                     device_id_type=MESH,
                 ).start()
 
+        each(owners, send)
+
     def share_sum(kind):
         @pl.when(owns)
         def _():
@@ -422,8 +441,7 @@
             part_own[kind] = total
             whole[kind, share_rows(mine), :] = total
 
-            @pl.loop(0, total_devices - 1)
-            def _(turn):
+            def send(turn):
                 peer = far_first(me, total_devices, turn)
                 pltpu.make_async_remote_copy(
                     src_ref=part_own.at[kind],
@@ -433,6 +451,8 @@
                     device_id=device_of(peer),
                     device_id_type=MESH,
                 ).start()
+
+            each(total_devices - 1, send)
 
     def await_sum(kind):
         @pl.when(owns)
@@ -495,7 +515,6 @@
     part[1, square_at : square_at + 1, :] = square_row
     send_parts(1)
     share_sum(0)
-    share_sum(1)
     await_sum(0)
 
     vertex_count = rows * total_devices
@@ -517,7 +536,7 @@
         work[top : top + 128, side : side + 128] = whole[0, at : at + 128, :] / vertex_count
         work[side : side + 128, top : top + 128] = jnp.zeros((128, 128), jnp.float32)
     work[:, feat:] = identity
-    factor_inverse(work, feat)
+    factor_inverse(work, feat, lambda: share_sum(1))
 
     inverse_ref[...] = work[:, feat:]
 

time: 35.2 us -> 35 us (level)
  no operation moved by 1% of the time
where the time goes in v5:
time: 35 us; the launch traced here: 34.9 us
  Pallas kernels  34.2 us (98%)
  between operations  0.64 us (2%)
    pallas_call x1, Pallas kernels, body(): pl.pallas_call(functools.partial(kernel, n_dom, n_sub, near_count // n_su...  32.5 us
    pallas_call x1, Pallas kernels, body(): pl.pallas_call(functools.partial(whiten, rows * total), out_shape=(jax.Sh...  1.73 us

profile of v5, /device:TPU:0, one launch (start us, length us, event | category | flops | bytes accessed | tf_op | source)
XLA Modules:
  0.0 34.9 jit_solution(9362405101434713140)
XLA Ops:
  0.6 32.5 %shard_map.104 = (bf16[1024,256]{1,0:T(8,128)(2,1)S(1)}, f32[256,256]{1,0:T(8,128)S(1)}, f32[272,128]{1,0:T(8,128)S(1)}) custom-call(bf16[8,128,256]{2,1,0:T(8,128)(2,1)} %bitcast.4, bf16[256,256]{1,0:T(8,128)(2,1)} %weight_in.1, s32[1,512]{1,0:T(1,128)} %bitcast.5, s32[1,128]{1,0:T(1,128)} %bitcast.6, s32[16]{0:T(128)} %dst_in.1, s32[8]{0:T(128)} %inner_in.1, ...), custom_call_target="tpu_custom_call" | custom-call | tf_op jit(solution)/shard_map/pallas_call | solution.py:639
  33.1 1.7 %shard_map.105 = (bf16[1024,256]{1,0:T(8,128)(2,1)}, f32[1,1]{1,0:T(1,128)}) custom-call(bf16[1024,256]{1,0:T(8,128)(2,1)S(1)} %get-tuple-element.7.hidden_ref, f32[256,256]{1,0:T(8,128)S(1)} %get-tuple-element.8.inverse_ref, f32[272,128]{1,0:T(8,128)S(1)} %get-tuple-element.9.sums_ref), custom_call_target="tpu_custom_call" | custom-call | tf_op jit(solution)/shard_map/pallas_call | solution.py:694
